TPU v7x, 256 devices: a whole 4x4x8 slice. The times are simulated.
256 devices in a mesh: seq: 16 (over z, core), feat: 16 (over y, x).
Axes of the slice: x: 4, y: 4, z: 8, core: 2. Of those that a mesh axis runs over, the one named last changes fastest.
Arguments:
- layer_inputs: bfloat16 [128, 256, 8192], P('seq', None, 'feat'), may hold values from -6 to 6
- out_grads: bfloat16 [128, 256, 28672], P('seq', None, 'feat'), may hold values from -6 to 6
- lengths: int32 [128], P('seq'), may hold values from 1 to 256, 20480 in all
- row_order: int32 [128], P('seq'), may hold values from 0 to 127, each once
- query_in: bfloat16 [8192, 512], P('feat'), may hold values from -0.005859375 to 0.005859375
- query_out: bfloat16 [28672, 512], P('feat'), may hold values from -0.0029296875 to 0.0029296875
Outputs:
- scores: float32 [128, 16], P('seq')
Inputs may be any that keep to these rules, and one draw needn't show every extreme that they name: `lengths`: slots at or past a sequence's length hold padding. `row_order`: each sequence number appears exactly once.
All inputs are finite; a program needn't handle non-finite values. No bound on the sum of `lengths` on one device may be relied on, other than what follows from the above.
Results may differ from a plain program's by a relative error of at most 0.018.
Values may be sent and summed in bfloat16 or wider, within the bound.
A program may use at most 64 MiB of HBM per device.

v0:
```python
import jax
import jax.numpy as jnp
from jax import lax
from jax.sharding import Mesh
from jax.sharding import PartitionSpec as P

Q = 16
R = 32
FEAT = ("feat_0", "feat_1")
SEQ = ("seq_0", "seq_1")


def split_up(array, dim, devices):
    lengths = array.shape
    parts = array.reshape(*lengths[:dim], devices, lengths[dim] // devices, *lengths[dim + 1 :])
    return jnp.moveaxis(parts, dim, 0)


def sent_and_summed(array, axis, dim):
    devices = lax.axis_size(axis)
    parts = lax.all_to_all(split_up(array, dim, devices), axis, 0, 0, tiled=True)
    return jnp.sum(parts.astype(jnp.float32), axis=0)


def sent_to_all(array, axis):
    copies = jnp.broadcast_to(array, (lax.axis_size(axis), *array.shape))
    return lax.all_to_all(copies, axis, split_axis=0, concat_axis=0, tiled=True)


def taken_together(array, axis):
    return sent_to_all(array, axis).sum(axis=0)


def one_axis_at_a_time(array, axes):
    far, near = axes
    nearer = taken_together(array, near)
    return taken_together(nearer, far)


def on_device(layer_inputs, out_grads, lengths, row_order, query_in, query_out):
    seq_dev, seq_len, width_in = layer_inputs.shape
    total_rows = seq_dev * seq_len
    columns = query_in.shape[1]
    flat_in = layer_inputs.reshape(total_rows, width_in)
    flat_out = out_grads.reshape(total_rows, out_grads.shape[2])
    projected = sent_and_summed(
        jnp.concatenate(
            [
                jnp.dot(flat_in, query_in, preferred_element_type=jnp.float32),
                jnp.dot(flat_out, query_out, preferred_element_type=jnp.float32),
            ],
            axis=1,
        ).astype(jnp.bfloat16),
        FEAT,
        0,
    )
    first_row = lax.axis_index(FEAT) * projected.shape[0]
    row_count = projected.shape[0]
    products = projected[:, :columns] * projected[:, columns:]
    row_index = first_row + jnp.arange(row_count, dtype=jnp.int32)
    seq_owner = row_index // seq_len
    position = row_index % seq_len
    membership = (seq_owner[None, :] == jnp.arange(seq_dev, dtype=jnp.int32)[:, None]) & (
        position[None, :] < lengths[:, None]
    )
    seq_sums = jnp.dot(membership.astype(jnp.float32), products, precision=lax.Precision.HIGHEST)
    local_scores = seq_sums.reshape(seq_dev, Q, R).sum(axis=2)
    all_seqs = seq_dev * lax.axis_size(SEQ)
    placed = lax.dynamic_update_slice_in_dim(
        jnp.zeros((all_seqs, Q), jnp.float32), local_scores, lax.axis_index(SEQ) * seq_dev, 0
    )
    gathered = one_axis_at_a_time(placed, (("seq_0", "seq_1", "feat_0"), "feat_1"))
    selector = (row_order[:, None] == jnp.arange(all_seqs, dtype=jnp.int32)[None, :]).astype(
        jnp.float32
    )
    return jnp.dot(selector, gathered, precision=lax.Precision.HIGHEST)


def solution(mesh):
    finer = Mesh(mesh.devices.reshape(8, 2, 4, 4), ("seq_0", "seq_1", "feat_0", "feat_1"))
    placed = (P(SEQ, None, FEAT), P(SEQ, None, FEAT), P(SEQ), P(SEQ), P(FEAT, None), P(FEAT, None))
    return jax.shard_map(
        on_device, mesh=finer, in_specs=placed, out_specs=P(SEQ, None), check_vma=False
    )
```

profile of v0, /device:TPU:1, one launch (start us, length us, event | category | flops | bytes accessed | tf_op | source)
XLA Modules:
  0.0 123.9 jit_solution(6134705944907058749)
XLA Ops:
  0.0 0.0 copy-start
  0.0 0.0 copy-start.2
  0.0 7.7 %convolution_convert_fusion = bf16[16,128,512]{2,1,0:T(8,128)(2,1)S(1)} fusion(bf16[16,128,1792]{2,1,0:T(8,128)(2,1)} %bitcast.12, bf16[1792,512]{1,0:T(8,128)(2,1)} %param.11), kind=kOutput, calls=%fused_computation.2 | convolution fusion | flops 3759144960 | bytes 11272192 | tf_op jit(solution)/shard_map/dot_general | solution.py:50
  7.7 0.0 copy-done
  7.7 0.0 copy-done.2
  7.7 1.2 %convolution_convert_fusion.1 = bf16[16,128,512]{2,1,0:T(8,128)(2,1)S(1)} fusion(bf16[16,128,512]{2,1,0:T(8,128)(2,1)S(1)} %bitcast.11, bf16[512,512]{1,0:T(8,128)(2,1)S(1)} %copy-done.2), kind=kOutput, calls=%fused_computation.3 | convolution fusion | flops 1074790400 | bytes 4718592 | tf_op jit(solution)/shard_map/dot_general | solution.py:49
  9.0 2.5 %pad_maximum_fusion = bf16[16,128,1024]{2,1,0:T(8,128)(2,1)} fusion(bf16[16,128,512]{2,1,0:T(8,128)(2,1)S(1)} %convolution_convert_fusion, bf16[16,128,512]{2,1,0:T(8,128)(2,1)S(1)} %convolution_convert_fusion.1), kind=kLoop, calls=%fused_computation.1 | loop fusion | flops 8388608 | bytes 8388608 | tf_op jit(solution)/shard_map/concatenate | solution.py:47
  11.5 7.6 %all-to-all-start = ((bf16[16,128,1024]{2,1,0:T(8,128)(2,1)}), bf16[16,128,1024]{2,1,0:T(8,128)(2,1)}, u32[]{:S(2)}, u32[]{:S(2)}) async-start(bf16[16,128,1024]{2,1,0:T(8,128)(2,1)} %pad_maximum_fusion), calls=%async_computation | async-start | bytes 8388608 | tf_op jit(solution)/shard_map/all_to_all | solution.py:21
  19.2 0.0 copy-start.1
  19.2 0.0 copy-start.3
  19.2 62.4 %all-to-all-done = bf16[16,128,1024]{2,1,0:T(8,128)(2,1)} async-done(((bf16[16,128,1024]{2,1,0:T(8,128)(2,1)}), bf16[16,128,1024]{2,1,0:T(8,128)(2,1)}, u32[]{:S(2)}, u32[]{:S(2)}) %all-to-all-start) | async-done | bytes 4194336 | tf_op jit(solution)/shard_map/all_to_all | solution.py:21
  81.6 3.1 %convert_reduce_fusion = f32[128,1024]{1,0:T(8,128)S(1)} fusion(bf16[16,128,1024]{2,1,0:T(8,128)(2,1)} %all-to-all-done), kind=kLoop, calls=%fused_computation | loop fusion | flops 4063232 | bytes 4718592 | tf_op jit(solution)/shard_map/reduce_sum | solution.py:22
  84.8 0.0 copy-done.1
  84.8 0.2 fusion.2
  85.0 0.1 reshape.46
  85.1 0.1 reduce_sum.37
  85.2 0.1 copy.7
  85.3 0.2 dynamic_update_slice.3
  85.5 6.7 %all_to_all.15 = f32[4,128,16]{1,2,0:T(8,128)S(1)} all-to-all(f32[4,128,16]{1,2,0:T(8,128)S(1)} %broadcast_in_dim.7), channel_id=1, replica_groups=mesh['seq_0'=8,'seq_1'=2,'feat_0'=4,'feat_1'=4] {'feat_1'}, dimensions={0} | all-to-all | bytes 65536 | tf_op jit(solution)/shard_map/all_to_all | solution.py:27
  92.2 30.8 %all_to_all.16 = f32[64,128,16]{1,2,0:T(8,128)S(1)} all-to-all(f32[64,128,16]{1,2,0:T(8,128)S(1)} %broadcast_in_dim.8), channel_id=1, replica_groups=mesh['seq_0'=8,'seq_1'=2,'feat_0'=4,'feat_1'=4] {'seq_0','seq_1','feat_0'}, dimensions={0} | all-to-all | bytes 1048576 | tf_op jit(solution)/shard_map/all_to_all | solution.py:27
  123.1 0.1 reduce_sum.39
  123.1 0.0 copy-done.3
  123.2 0.8 fusion.4
  (5 shorter events, 0.1 us)
Async XLA Ops:
  0.0 7.7 %copy-start = (bf16[8,256,512]{2,1,0:T(8,128)(2,1)S(1)}, bf16[8,256,512]{2,1,0:T(8,128)(2,1)}, u32[]{:S(2)}) copy-start(bf16[8,256,512]{2,1,0:T(8,128)(2,1)} %param.6) | copy-start | bytes 6291460
  0.0 7.7 %copy-start.2 = (bf16[512,512]{1,0:T(8,128)(2,1)S(1)}, bf16[512,512]{1,0:T(8,128)(2,1)}, u32[]{:S(2)}) copy-start(bf16[512,512]{1,0:T(8,128)(2,1)} %param.10) | copy-start | bytes 1572868
  11.5 70.1 %all-to-all-start = ((bf16[16,128,1024]{2,1,0:T(8,128)(2,1)}), bf16[16,128,1024]{2,1,0:T(8,128)(2,1)}, u32[]{:S(2)}, u32[]{:S(2)}) async-start(bf16[16,128,1024]{2,1,0:T(8,128)(2,1)} %pad_maximum_fusion), calls=%async_computation | async-start | bytes 8388608 | tf_op jit(solution)/shard_map/all_to_all | solution.py:21
  19.2 65.6 %copy-start.1 = (s32[8]{0:T(128)S(1)}, s32[8]{0:T(128)}, u32[]{:S(2)}) copy-start(s32[8]{0:T(128)} %param.8) | copy-start | bytes 100
  19.2 104.0 %copy-start.3 = (s32[8]{0:T(128)S(1)}, s32[8]{0:T(128)}, u32[]{:S(2)}) copy-start(s32[8]{0:T(128)} %param.9) | copy-start | bytes 100
where the time goes:
time: 124 us
  waiting for transfers between devices  62.4 us (50%)
  blocking collectives  37.5 us (30%)
  matrix products  9.96 us (8%)
  starting transfers between devices  7.63 us (6%)
  other arithmetic  5.86 us (5%)
    all_to_all x1, waiting for transfers between devices, sent_and_summed(): lax.all_to_all(split_up(array, dim, devices), axis, 0, 0, tiled=True)  62.4 us
    all_to_all x2, blocking collectives, sent_to_all(): return lax.all_to_all(copies, axis, split_axis=0, concat_axis=0, tiled=True)  37.5 us
    dot_general x1, matrix products, on_device(): jnp.dot(flat_out, query_out, preferred_element_type=jnp.float32)  7.7 us
    all_to_all x1, starting transfers between devices, sent_and_summed(): lax.all_to_all(split_up(array, dim, devices), axis, 0, 0, tiled=True)  7.63 us
    reduce_sum x1, other arithmetic, sent_and_summed(): return jnp.sum(parts.astype(jnp.float32), axis=0)  3.15 us
    concatenate x1, other arithmetic, on_device(): jnp.concatenate([jnp.dot(flat_in, query_in, preferred_element_type=jnp.fl...  2.53 us
  transfers between devices with their start and end apart: 1, of which 1 were waited for; matrix products, arithmetic and copies ran while one was open for 0% of the time, Pallas kernels for 0%

commit v1 on v0

v1 whole, which is shorter than its diff:
```python
import functools

import jax
import jax.numpy as jnp
from jax import lax
from jax.experimental import pallas as pl
from jax.experimental.pallas import tpu as pltpu
from jax.sharding import PartitionSpec as P

Q = 16
R = 32
SIDE = 4
LANES = 128
OFFS = (2, 1, 3, 0)
BF16 = jnp.bfloat16
F32 = jnp.float32


def kernel(n_seq, lengths, row_order, li, og, qi, qo, out,
           xb, gb, wi, wo, part, rec1, acc1, mid, rec2, acc2, tile, gz, mine, gp,
           load_sem, s1_send, s1_recv, s2_send, s2_recv, gz_sem, gp_sem):
    n_feat = SIDE * SIDE
    me_s = lax.axis_index("seq")
    me_f = lax.axis_index("feat")
    y = me_f // SIDE
    x = me_f % SIDE
    rows = xb.shape[2]
    seq_dev = li.shape[0]

    def neighbour(axis, step):
        if axis == 0:
            return y * SIDE + lax.rem(x + step, SIDE)
        return lax.rem(y + step, SIDE) * SIDE + x

    pos = (x, y)

    barrier = pltpu.get_barrier_semaphore()
    for d in range(1, n_feat):
        pl.semaphore_signal(barrier, inc=1, device_id={"feat": lax.rem(me_f + d, n_feat)},
                            device_id_type=pl.DeviceIdType.MESH)
    for d in range(1, n_seq):
        pl.semaphore_signal(barrier, inc=1, device_id={"seq": lax.rem(me_s + d, n_seq)},
                            device_id_type=pl.DeviceIdType.MESH)

    def seq_of(h, t):
        return h * SIDE + lax.rem(pos[1 - h] + OFFS[t], SIDE)

    def load_x(h, t):
        return pltpu.make_async_copy(li.at[seq_of(h, t)], xb.at[h, t], load_sem.at[2 + h * 8 + t * 2])

    def load_g(h, t):
        return pltpu.make_async_copy(og.at[seq_of(h, t)], gb.at[h, t], load_sem.at[3 + h * 8 + t * 2])

    load_wi = pltpu.make_async_copy(qi, wi, load_sem.at[0])
    load_wo = pltpu.make_async_copy(qo, wo, load_sem.at[1])
    load_wi.start()
    load_x(0, 0).start()
    load_x(1, 0).start()
    load_wo.start()
    load_g(0, 0).start()
    load_g(1, 0).start()
    for h in range(2):
        load_x(h, 1).start()
        load_g(h, 1).start()

    def send(src, dst, ssem, rsem, target):
        copy = pltpu.make_async_remote_copy(
            src_ref=src, dst_ref=dst, send_sem=ssem, recv_sem=rsem,
            device_id={"feat": target}, device_id_type=pl.DeviceIdType.MESH)
        return copy

    def ring_copy(axis, slot, src, rec, ssem, rsem):
        step = 1 if slot in (0, 2, 5) else SIDE - 1
        return send(src, rec.at[slot], ssem.at[slot], rsem.at[slot], neighbour(axis, step))

    def tile_in(h, t, step):
        return part.at[h, t, lax.rem(pos[h] + step, SIDE)]

    def tile_out(h, t, step):
        return part.at[h, t, SIDE + lax.rem(pos[h] + step, SIDE)]

    def copy1(h, t, slot):
        if slot >= 4:
            src = acc1.at[h, t, slot - 4]
        elif slot in (0, 3):
            src = tile_in(h, t, 1 if slot == 0 else 2)
        else:
            src = tile_out(h, t, 3 if slot == 1 else 2)
        return ring_copy(h, slot, src, rec1.at[h, t], s1_send.at[h, t], s1_recv.at[h, t])

    def copy2(h, slot):
        src = (mid.at[h, 1, 0], mid.at[h, 2, 1], mid.at[h, 0, 1], mid.at[h, 0, 0], acc2.at[h, 0], acc2.at[h, 1])[slot]
        return ring_copy(1 - h, slot, src, rec2.at[h], s2_send.at[h], s2_recv.at[h])

    def added(*refs):
        total = refs[0][...].astype(F32)
        for ref in refs[1:]:
            total = total + ref[...].astype(F32)
        return total

    def compute_in(h, t):
        load_x(h, t).wait()
        value = jnp.dot(xb[h, t], wi[...], preferred_element_type=F32).astype(BF16)
        for c in range(SIDE):
            part[h, t, c] = value[:, c * LANES:(c + 1) * LANES]

    def compute_out(h, t):
        load_g(h, t).wait()
        value = jnp.dot(gb[h, t], wo[...], preferred_element_type=F32).astype(BF16)
        for c in range(SIDE):
            part[h, t, SIDE + c] = value[:, c * LANES:(c + 1) * LANES]

    def accumulate1(h, t):
        copy1(h, t, 3).wait_recv()
        acc1[h, t, 0] = added(tile_in(h, t, 3), rec1.at[h, t, 3]).astype(BF16)
        copy1(h, t, 4).start()
        copy1(h, t, 2).wait_recv()
        acc1[h, t, 1] = added(tile_out(h, t, 1), rec1.at[h, t, 2]).astype(BF16)
        copy1(h, t, 5).start()

    def final1(h, t):
        copy1(h, t, 0).wait_recv()
        copy1(h, t, 4).wait_recv()
        mid[h, t, 0] = added(tile_in(h, t, 0), rec1.at[h, t, 0], rec1.at[h, t, 4]).astype(BF16)
        copy1(h, t, 1).wait_recv()
        copy1(h, t, 5).wait_recv()
        mid[h, t, 1] = added(tile_out(h, t, 0), rec1.at[h, t, 1], rec1.at[h, t, 5]).astype(BF16)

    def step(t):
        for h in range(2):
            compute_in(h, t)
            if t == 0 and h == 0:
                pl.semaphore_wait(barrier, n_feat - 1 + n_seq - 1)
            copy1(h, t, 3).start()
            copy1(h, t, 0).start()
        if t == 0:
            load_wo.wait()
        for h in range(2):
            compute_out(h, t)
            copy1(h, t, 2).start()
            copy1(h, t, 1).start()
        if t + 2 < SIDE:
            for h in range(2):
                load_x(h, t + 2).start()
                load_g(h, t + 2).start()

    load_wi.wait()
    step(0)
    step(1)
    for h in range(2):
        accumulate1(h, 0)
    step(2)
    for h in range(2):
        accumulate1(h, 1)
    for h in range(2):
        final1(h, 0)
        copy2(h, 3).start()
        copy2(h, 2).start()
    step(3)
    for h in range(2):
        accumulate1(h, 2)
    for h in range(2):
        final1(h, 1)
        copy2(h, 0).start()
    for h in range(2):
        accumulate1(h, 3)
    for h in range(2):
        copy2(h, 2).wait_recv()
        acc2[h, 1] = added(mid.at[h, 1, 1], rec2.at[h, 2]).astype(BF16)
        copy2(h, 5).start()
    for h in range(2):
        final1(h, 2)
        copy2(h, 1).start()
        copy2(h, 3).wait_recv()
        acc2[h, 0] = added(mid.at[h, 2, 0], rec2.at[h, 3]).astype(BF16)
        copy2(h, 4).start()

    row = lax.broadcasted_iota(jnp.int32, (seq_dev, rows), 1)
    seq_id = lax.broadcasted_iota(jnp.int32, (seq_dev, rows), 0)
    lane_from = lax.broadcasted_iota(jnp.int32, (LANES, LANES), 0)
    lane_to = lax.broadcasted_iota(jnp.int32, (LANES, LANES), 1)
    total = None
    for h in range(2):
        copy1(h, 3, 0).wait_recv()
        copy1(h, 3, 4).wait_recv()
        copy2(h, 0).wait_recv()
        copy2(h, 4).wait_recv()
        both_in = added(tile_in(h, 3, 0), rec1.at[h, 3, 0], rec1.at[h, 3, 4], rec2.at[h, 0], rec2.at[h, 4])
        copy1(h, 3, 1).wait_recv()
        copy1(h, 3, 5).wait_recv()
        copy2(h, 1).wait_recv()
        copy2(h, 5).wait_recv()
        both_out = added(tile_out(h, 3, 0), rec1.at[h, 3, 1], rec1.at[h, 3, 5], rec2.at[h, 1], rec2.at[h, 5])
        products = both_in * both_out
        which = seq_of(h, 3)
        live = (seq_id == which) & (row < lengths[which])
        sums = jnp.dot(live.astype(F32), products, precision=lax.Precision.HIGHEST, preferred_element_type=F32)
        place = (lane_to == pos[h] * (LANES // R) + lane_from // R).astype(F32)
        scored = jnp.dot(sums, place, precision=lax.Precision.HIGHEST, preferred_element_type=F32)
        total = scored if total is None else total + scored
    tile[...] = total
    gz[me_s] = total

    def spread_z(d):
        return pltpu.make_async_remote_copy(
            src_ref=tile, dst_ref=gz.at[me_s], send_sem=gz_sem.at[0], recv_sem=gz_sem.at[1],
            device_id={"seq": lax.rem(me_s + d, n_seq)}, device_id_type=pl.DeviceIdType.MESH)

    def spread_plane(d):
        return pltpu.make_async_remote_copy(
            src_ref=mine, dst_ref=gp.at[me_f], send_sem=gp_sem.at[0], recv_sem=gp_sem.at[1],
            device_id={"feat": lax.rem(me_f + d, n_feat)}, device_id_type=pl.DeviceIdType.MESH)

    def all_of(ref, sem, n, axis):
        return pltpu.make_async_remote_copy(
            src_ref=ref.at[pl.ds(0, n)], dst_ref=ref.at[pl.ds(0, n)], send_sem=sem.at[0], recv_sem=sem.at[1],
            device_id={axis: lax.axis_index(axis)}, device_id_type=pl.DeviceIdType.MESH)

    for d in range(1, n_seq):
        spread_z(d).start()
    wanted = jnp.zeros((seq_dev, seq_dev * n_seq), jnp.int32)
    out_row = lax.broadcasted_iota(jnp.int32, wanted.shape, 0)
    for i in range(seq_dev):
        wanted = jnp.where(out_row == i, row_order[i], wanted)
    picked = (wanted == lax.broadcasted_iota(jnp.int32, wanted.shape, 1)).astype(F32)
    if n_seq > 1:
        all_of(gz, gz_sem, n_seq - 1, "seq").wait_recv()
    every = gz[...].reshape(n_seq * seq_dev, LANES)
    own = jnp.dot(picked, every, precision=lax.Precision.HIGHEST, preferred_element_type=F32)
    mine[...] = own
    gp[me_f] = own
    for d in range(1, n_feat):
        spread_plane(d).start()
    for h in range(2):
        for t in range(SIDE):
            for slot in range(6):
                copy1(h, t, slot).wait_send()
        for slot in range(6):
            copy2(h, slot).wait_send()
    if n_seq > 1:
        all_of(gz, gz_sem, n_seq - 1, "seq").wait_send()
    all_of(gp, gp_sem, n_feat - 1, "feat").wait_recv()
    summed = gp[0]
    for f in range(1, n_feat):
        summed = summed + gp[f]
    out[...] = summed[:, :Q]
    all_of(gp, gp_sem, n_feat - 1, "feat").wait_send()


def on_device(n_seq, layer_inputs, out_grads, lengths, row_order, query_in, query_out):
    seq_dev, rows, width_in = layer_inputs.shape
    width_out = out_grads.shape[2]
    columns = query_in.shape[1]
    n_feat = SIDE * SIDE
    smem = pl.BlockSpec(memory_space=pltpu.SMEM)
    hbm = pl.BlockSpec(memory_space=pl.ANY)
    tile_of = (rows, LANES)
    return pl.pallas_call(
        functools.partial(kernel, n_seq),
        out_shape=jax.ShapeDtypeStruct((seq_dev, Q), F32),
        in_specs=[smem, smem, hbm, hbm, hbm, hbm],
        out_specs=pl.BlockSpec(memory_space=pltpu.VMEM),
        scratch_shapes=[
            pltpu.VMEM((2, SIDE, rows, width_in), BF16),
            pltpu.VMEM((2, SIDE, rows, width_out), BF16),
            pltpu.VMEM((width_in, columns), BF16),
            pltpu.VMEM((width_out, columns), BF16),
            pltpu.VMEM((2, SIDE, 2 * SIDE, *tile_of), BF16),
            pltpu.VMEM((2, SIDE, 6, *tile_of), BF16),
            pltpu.VMEM((2, SIDE, 2, *tile_of), BF16),
            pltpu.VMEM((2, SIDE, 2, *tile_of), BF16),
            pltpu.VMEM((2, 6, *tile_of), BF16),
            pltpu.VMEM((2, 2, *tile_of), BF16),
            pltpu.VMEM((seq_dev, LANES), F32),
            pltpu.VMEM((n_seq, seq_dev, LANES), F32),
            pltpu.VMEM((seq_dev, LANES), F32),
            pltpu.VMEM((n_feat, seq_dev, LANES), F32),
            pltpu.SemaphoreType.DMA((18,)),
            pltpu.SemaphoreType.DMA((2, SIDE, 6)),
            pltpu.SemaphoreType.DMA((2, SIDE, 6)),
            pltpu.SemaphoreType.DMA((2, 6)),
            pltpu.SemaphoreType.DMA((2, 6)),
            pltpu.SemaphoreType.DMA((2,)),
            pltpu.SemaphoreType.DMA((2,)),
        ],
        compiler_params=pltpu.CompilerParams(collective_id=0, has_side_effects=True, vmem_limit_bytes=60 * 1024 * 1024),
        name="scores",
    )(lengths, row_order, layer_inputs, out_grads, query_in, query_out)


def solution(mesh):
    placed = (P("seq", None, "feat"), P("seq", None, "feat"), P("seq"), P("seq"), P("feat", None), P("feat", None))
    return jax.shard_map(
        functools.partial(on_device, mesh.shape["seq"]),
        mesh=mesh, in_specs=placed, out_specs=P("seq", None), check_vma=False)
```

time: 124 us -> 49.1 us (0.40)
  waiting for transfers between devices: 62.4 us -> 0 us
  Pallas kernels: 0 us -> 47.7 us
  blocking collectives: 37.5 us -> 0 us
  matrix products: 9.96 us -> 0 us
  starting transfers between devices: 7.63 us -> 0 us
  other arithmetic: 5.86 us -> 0 us
    all_to_all x1 -> x0, waiting for transfers between devices: 62.4 us -> none  [sent_and_summed(): lax.all_to_all(split_up(array, dim, devices), axis, 0, 0, tiled=True)]
    pallas_call x0 -> x1, Pallas kernels: none -> 47.7 us  [on_device(): pl.pallas_call(functools.partial(kernel, n_seq), out_shape=jax.ShapeDtype...]
    all_to_all x2 -> x0, blocking collectives: 37.5 us -> none  [sent_to_all(): return lax.all_to_all(copies, axis, split_axis=0, concat_axis=0, tiled=True)]
    dot_general x4 -> x0, matrix products: 9.96 us -> none  [the longest x1 7.7 us: on_device(): jnp.dot(flat_out, query_out, preferred_element_type=jnp.float32)]
    all_to_all x1 -> x0, starting transfers between devices: 7.63 us -> none  [sent_and_summed(): lax.all_to_all(split_up(array, dim, devices), axis, 0, 0, tiled=True)]
    reduce_sum x4 -> x0, other arithmetic: 3.32 us -> none  [the longest x1 3.15 us: sent_and_summed(): return jnp.sum(parts.astype(jnp.float32), axis=0)]
    concatenate x1 -> x0, other arithmetic: 2.53 us -> none  [on_device(): jnp.concatenate([jnp.dot(flat_in, query_in, preferred_element_type=jnp.fl...]
    unnamed x8 -> x1, local copies, waits for them, and re-layouts: 0.02 us -> 1.28 us
  transfers between devices with their start and end apart: 1 -> 0, of which waited for: 1 -> 0; matrix products, arithmetic and copies ran while one was open for 0% -> 0% of each run, Pallas kernels for 0% -> 0%
where the time goes in v1:
time: 49.1 us; the launch traced here: 49 us
  Pallas kernels  47.7 us (97%)
  local copies, waits for them, and re-layouts  1.28 us (3%)
    pallas_call x1, Pallas kernels, on_device(): pl.pallas_call(functools.partial(kernel, n_seq), out_shape=jax.ShapeDtype...  47.7 us
    unnamed x1, local copies, waits for them, and re-layouts  1.28 us

profile of v1, /device:TPU:1, one launch (start us, length us, event | category | flops | bytes accessed | tf_op | source)
XLA Modules:
  0.0 49.0 jit_solution(1996359956550265360)
XLA Ops:
  0.0 47.7 %scores.1 = f32[8,16]{1,0:T(8,128)} custom-call(s32[8]{0:T(128)} %lengths.1, s32[8]{0:T(128)} %row_order.1, bf16[8,256,512]{2,1,0:T(8,128)(2,1)} %li.1, bf16[8,256,1792]{2,1,0:T(8,128)(2,1)} %og.1, bf16[512,512]{1,0:T(8,128)(2,1)} %qi.1, bf16[1792,512]{1,0:T(8,128)(2,1)} %qo.1), custom_call_target="tpu_custom_call" | custom-call | tf_op jit(solution)/shard_map/scores/pallas_call | solution.py:258
  47.7 1.3 %copy.8 = f32[8,16]{1,0:T(8,128)} copy(f32[8,16]{1,0:T(8,128)} %scores.1) | data formatting | bytes 1024

commit v2 on v1

--- a/solution.py
+++ b/solution.py
@@ -11,14 +11,15 @@
 R = 32
 SIDE = 4
 LANES = 128
+SUBLANES = 8
 OFFS = (2, 1, 3, 0)
 BF16 = jnp.bfloat16
 F32 = jnp.float32
 
 
-def kernel(n_seq, lengths, row_order, li, og, qi, qo, out,
-           xb, gb, wi, wo, part, rec1, acc1, mid, rec2, acc2, tile, gz, mine, gp,
-           load_sem, s1_send, s1_recv, s2_send, s2_recv, gz_sem, gp_sem):
+def kernel(n_seq, lengths_hbm, order_hbm, li, og, qi, qo, out,
+           xb, gb, wi, wo, part, rec1, acc1, mid, rec2, acc2, early, tile, gz, mine, gp, lengths, row_order,
+           load_sem, s1_send, s1_recv, s2_send, s2_recv, gz_sem, gp_sem, known):
     n_feat = SIDE * SIDE
     me_s = lax.axis_index("seq")
     me_f = lax.axis_index("feat")
@@ -34,16 +35,36 @@
 
     pos = (x, y)
 
+    n_z = n_seq // 2
+    z = me_s // 2
+    core = lax.rem(me_s, 2)
+    rounds = n_z // 2
+    above_below = [{"seq": lax.rem(me_s + d, n_seq)} for d in (2, n_seq - 2)] if n_z > 1 else []
+    nearby = [{"feat": neighbour(axis, d)} for axis in range(2) for d in (1, SIDE - 1)] + above_below
+    if n_seq > 1:
+        nearby.append({"seq": me_s + 1 - 2 * core})
+
+    def signal(sem, target):
+        pl.semaphore_signal(sem, inc=1, device_id=target, device_id_type=pl.DeviceIdType.MESH)
+
     barrier = pltpu.get_barrier_semaphore()
-    for d in range(1, n_feat):
-        pl.semaphore_signal(barrier, inc=1, device_id={"feat": lax.rem(me_f + d, n_feat)},
-                            device_id_type=pl.DeviceIdType.MESH)
-    for d in range(1, n_seq):
-        pl.semaphore_signal(barrier, inc=1, device_id={"seq": lax.rem(me_s + d, n_seq)},
-                            device_id_type=pl.DeviceIdType.MESH)
+    for target in nearby:
+        signal(barrier, target)
+
+    def tell(r):
+        if r < rounds:
+            for target in above_below:
+                signal(known.at[r], target)
+
+    def heard(r):
+        if r < rounds:
+            pl.semaphore_wait(known.at[r], 2)
 
     def seq_of(h, t):
         return h * SIDE + lax.rem(pos[1 - h] + OFFS[t], SIDE)
+
+    load_lengths = pltpu.make_async_copy(lengths_hbm, lengths, load_sem.at[18])
+    load_order = pltpu.make_async_copy(order_hbm, row_order, load_sem.at[19])
 
     def load_x(h, t):
         return pltpu.make_async_copy(li.at[seq_of(h, t)], xb.at[h, t], load_sem.at[2 + h * 8 + t * 2])
@@ -126,44 +147,71 @@
         copy1(h, t, 5).wait_recv()
         mid[h, t, 1] = added(tile_out(h, t, 0), rec1.at[h, t, 1], rec1.at[h, t, 5]).astype(BF16)
 
-    def step(t):
+    def send_in(t):
         for h in range(2):
-            compute_in(h, t)
-            if t == 0 and h == 0:
-                pl.semaphore_wait(barrier, n_feat - 1 + n_seq - 1)
             copy1(h, t, 3).start()
             copy1(h, t, 0).start()
-        if t == 0:
-            load_wo.wait()
+
+    def send_out(t):
         for h in range(2):
-            compute_out(h, t)
             copy1(h, t, 2).start()
             copy1(h, t, 1).start()
-        if t + 2 < SIDE:
-            for h in range(2):
-                load_x(h, t + 2).start()
-                load_g(h, t + 2).start()
+
+    def load_later(t):
+        for h in range(2):
+            load_x(h, t).start()
+            load_g(h, t).start()
 
     load_wi.wait()
-    step(0)
-    step(1)
+    for h in range(2):
+        compute_in(h, 0)
+    pl.semaphore_wait(barrier, len(nearby))
+    send_in(0)
+    tell(0)
+    load_wo.wait()
+    for h in range(2):
+        compute_out(h, 0)
+    send_out(0)
+    load_later(2)
+    load_lengths.start()
+    load_order.start()
+    for h in range(2):
+        compute_in(h, 1)
+    send_in(1)
+    for h in range(2):
+        compute_out(h, 1)
+    send_out(1)
+    load_later(3)
+    heard(0)
+    tell(1)
     for h in range(2):
         accumulate1(h, 0)
-    step(2)
+    for h in range(2):
+        compute_in(h, 2)
+    send_in(2)
+    for h in range(2):
+        compute_out(h, 2)
+    send_out(2)
+    heard(1)
+    tell(2)
     for h in range(2):
         accumulate1(h, 1)
     for h in range(2):
         final1(h, 0)
         copy2(h, 3).start()
         copy2(h, 2).start()
-    step(3)
+    heard(2)
+    tell(3)
+    for h in range(2):
+        compute_in(h, 3)
+        compute_out(h, 3)
     for h in range(2):
         accumulate1(h, 2)
+    send_in(3)
+    send_out(3)
     for h in range(2):
         final1(h, 1)
         copy2(h, 0).start()
-    for h in range(2):
-        accumulate1(h, 3)
     for h in range(2):
         copy2(h, 2).wait_recv()
         acc2[h, 1] = added(mid.at[h, 1, 1], rec2.at[h, 2]).astype(BF16)
@@ -174,76 +222,107 @@
         copy2(h, 3).wait_recv()
         acc2[h, 0] = added(mid.at[h, 2, 0], rec2.at[h, 3]).astype(BF16)
         copy2(h, 4).start()
-
-    row = lax.broadcasted_iota(jnp.int32, (seq_dev, rows), 1)
-    seq_id = lax.broadcasted_iota(jnp.int32, (seq_dev, rows), 0)
+    for h in range(2):
+        accumulate1(h, 3)
+    for h in range(2):
+        for side, own in enumerate((tile_in(h, 3, 0), tile_out(h, 3, 0))):
+            copy1(h, 3, side).wait_recv()
+            copy2(h, side).wait_recv()
+            early[h, side] = added(own, rec1.at[h, 3, side], rec2.at[h, side])
+    for h in range(2):
+        for side in range(2):
+            copy2(h, 4 + side).wait_recv()
+            early[h, side] = added(early.at[h, side], rec2.at[h, 4 + side])
+    heard(3)
+    load_lengths.wait()
+    load_order.wait()
+
+    row = lax.broadcasted_iota(jnp.int32, (rows, LANES), 0)
+    slot_row = lax.broadcasted_iota(jnp.int32, (SUBLANES, LANES), 0)
+    sums = jnp.zeros((SUBLANES, LANES), F32)
+    for h in range(2):
+        live = row < lengths[seq_of(h, 3)]
+        copy1(h, 3, 4).wait_recv()
+        copy1(h, 3, 5).wait_recv()
+        products = added(early.at[h, 0], rec1.at[h, 3, 4]) * added(early.at[h, 1], rec1.at[h, 3, 5])
+        column_sums = jnp.sum(jnp.where(live, products, 0.0), axis=0, keepdims=True)
+        sums = jnp.where(slot_row == h, column_sums, sums)
+    high = sums.astype(BF16).astype(F32)
+    middle = (sums - high).astype(BF16).astype(F32)
+    low = sums - high - middle
+    pieces = jnp.concatenate([high, middle, low], axis=0).astype(BF16)
     lane_from = lax.broadcasted_iota(jnp.int32, (LANES, LANES), 0)
     lane_to = lax.broadcasted_iota(jnp.int32, (LANES, LANES), 1)
-    total = None
-    for h in range(2):
-        copy1(h, 3, 0).wait_recv()
-        copy1(h, 3, 4).wait_recv()
-        copy2(h, 0).wait_recv()
-        copy2(h, 4).wait_recv()
-        both_in = added(tile_in(h, 3, 0), rec1.at[h, 3, 0], rec1.at[h, 3, 4], rec2.at[h, 0], rec2.at[h, 4])
-        copy1(h, 3, 1).wait_recv()
-        copy1(h, 3, 5).wait_recv()
-        copy2(h, 1).wait_recv()
-        copy2(h, 5).wait_recv()
-        both_out = added(tile_out(h, 3, 0), rec1.at[h, 3, 1], rec1.at[h, 3, 5], rec2.at[h, 1], rec2.at[h, 5])
-        products = both_in * both_out
-        which = seq_of(h, 3)
-        live = (seq_id == which) & (row < lengths[which])
-        sums = jnp.dot(live.astype(F32), products, precision=lax.Precision.HIGHEST, preferred_element_type=F32)
-        place = (lane_to == pos[h] * (LANES // R) + lane_from // R).astype(F32)
-        scored = jnp.dot(sums, place, precision=lax.Precision.HIGHEST, preferred_element_type=F32)
-        total = scored if total is None else total + scored
-    tile[...] = total
-    gz[me_s] = total
-
-    def spread_z(d):
+    per_chunk = LANES // R
+    group = (lane_from // R == lax.rem(lane_to, per_chunk)).astype(F32).astype(BF16)
+    grouped = jnp.dot(pieces, group, preferred_element_type=F32)
+    grouped = grouped[:SUBLANES] + grouped[SUBLANES:2 * SUBLANES] + grouped[2 * SUBLANES:]
+    lane = lax.broadcasted_iota(jnp.int32, (SUBLANES, LANES), 1)
+    chunk = lax.rem(lane, Q) // per_chunk
+    scored = jnp.where(chunk == jnp.where(slot_row == 0, x, y), grouped, 0.0)[:2]
+    tile[...] = scored
+    gz[me_s] = scored
+
+    def spread_z(dz, flip):
+        target = lax.rem(z + dz, n_z) * 2 + (1 - core if flip else core)
         return pltpu.make_async_remote_copy(
             src_ref=tile, dst_ref=gz.at[me_s], send_sem=gz_sem.at[0], recv_sem=gz_sem.at[1],
-            device_id={"seq": lax.rem(me_s + d, n_seq)}, device_id_type=pl.DeviceIdType.MESH)
-
-    def spread_plane(d):
+            device_id={"seq": target}, device_id_type=pl.DeviceIdType.MESH)
+
+    def spread_plane(dy, dx):
+        target = lax.rem(y + dy, SIDE) * SIDE + lax.rem(x + dx, SIDE)
         return pltpu.make_async_remote_copy(
             src_ref=mine, dst_ref=gp.at[me_f], send_sem=gp_sem.at[0], recv_sem=gp_sem.at[1],
-            device_id={"feat": lax.rem(me_f + d, n_feat)}, device_id_type=pl.DeviceIdType.MESH)
+            device_id={"feat": target}, device_id_type=pl.DeviceIdType.MESH)
 
     def all_of(ref, sem, n, axis):
         return pltpu.make_async_remote_copy(
             src_ref=ref.at[pl.ds(0, n)], dst_ref=ref.at[pl.ds(0, n)], send_sem=sem.at[0], recv_sem=sem.at[1],
             device_id={axis: lax.axis_index(axis)}, device_id_type=pl.DeviceIdType.MESH)
 
-    for d in range(1, n_seq):
-        spread_z(d).start()
-    wanted = jnp.zeros((seq_dev, seq_dev * n_seq), jnp.int32)
-    out_row = lax.broadcasted_iota(jnp.int32, wanted.shape, 0)
-    for i in range(seq_dev):
-        wanted = jnp.where(out_row == i, row_order[i], wanted)
-    picked = (wanted == lax.broadcasted_iota(jnp.int32, wanted.shape, 1)).astype(F32)
-    if n_seq > 1:
-        all_of(gz, gz_sem, n_seq - 1, "seq").wait_recv()
-    every = gz[...].reshape(n_seq * seq_dev, LANES)
-    own = jnp.dot(picked, every, precision=lax.Precision.HIGHEST, preferred_element_type=F32)
-    mine[...] = own
-    gp[me_f] = own
-    for d in range(1, n_feat):
-        spread_plane(d).start()
+    def hops(d, size):
+        return min(d, size - d)
+
+    far_first = sorted(((hops(dz, n_z), flip, dz) for dz in range(n_z) for flip in range(2)), reverse=True)
+    for _, flip, dz in far_first:
+        if dz or flip:
+            if n_seq > 1:
+                spread_z(dz, flip).start()
     for h in range(2):
         for t in range(SIDE):
             for slot in range(6):
                 copy1(h, t, slot).wait_send()
         for slot in range(6):
             copy2(h, slot).wait_send()
+    one_lane = lax.broadcasted_iota(jnp.int32, (1, LANES), 1) // Q
+    picks = []
+    for i in range(seq_dev):
+        wanted = row_order[i]
+        within = lax.rem(wanted, seq_dev)
+        half = within // SIDE
+        ours = lax.rem(within, SIDE) == jnp.where(half == 0, y, x)
+        picks.append((wanted // seq_dev, half, jnp.where(ours, i, -1)))
+    if n_seq > 1:
+        all_of(gz, gz_sem, n_seq - 1, "seq").wait_recv()
+    packed = jnp.zeros((1, LANES), F32)
+    for who, half, place in picks:
+        packed = jnp.where(one_lane == place, gz[who, pl.ds(half, 1), :], packed)
+    mine[...] = packed
+    gp[me_f] = packed
+    far_first = sorted(((hops(dy, SIDE) + hops(dx, SIDE), dy, dx) for dy in range(SIDE) for dx in range(SIDE)), reverse=True)
+    for _, dy, dx in far_first[:-1]:
+        spread_plane(dy, dx).start()
     if n_seq > 1:
         all_of(gz, gz_sem, n_seq - 1, "seq").wait_send()
     all_of(gp, gp_sem, n_feat - 1, "feat").wait_recv()
     summed = gp[0]
     for f in range(1, n_feat):
         summed = summed + gp[f]
-    out[...] = summed[:, :Q]
+    spread = jnp.broadcast_to(summed, (seq_dev, LANES))
+    lined = spread
+    for i in range(1, seq_dev):
+        lined = jnp.where(slot_row == i, pltpu.roll(spread, LANES - i * Q, 1), lined)
+    out[...] = lined[:, :Q]
     all_of(gp, gp_sem, n_feat - 1, "feat").wait_send()
 
 
@@ -252,13 +331,12 @@
     width_out = out_grads.shape[2]
     columns = query_in.shape[1]
     n_feat = SIDE * SIDE
-    smem = pl.BlockSpec(memory_space=pltpu.SMEM)
     hbm = pl.BlockSpec(memory_space=pl.ANY)
     tile_of = (rows, LANES)
     return pl.pallas_call(
         functools.partial(kernel, n_seq),
-        out_shape=jax.ShapeDtypeStruct((seq_dev, Q), F32),
-        in_specs=[smem, smem, hbm, hbm, hbm, hbm],
+        out_shape=pltpu.VMEM((seq_dev, Q), F32),
+        in_specs=[hbm] * 6,
         out_specs=pl.BlockSpec(memory_space=pltpu.VMEM),
         scratch_shapes=[
             pltpu.VMEM((2, SIDE, rows, width_in), BF16),
@@ -271,17 +349,21 @@
             pltpu.VMEM((2, SIDE, 2, *tile_of), BF16),
             pltpu.VMEM((2, 6, *tile_of), BF16),
             pltpu.VMEM((2, 2, *tile_of), BF16),
-            pltpu.VMEM((seq_dev, LANES), F32),
-            pltpu.VMEM((n_seq, seq_dev, LANES), F32),
-            pltpu.VMEM((seq_dev, LANES), F32),
-            pltpu.VMEM((n_feat, seq_dev, LANES), F32),
-            pltpu.SemaphoreType.DMA((18,)),
+            pltpu.VMEM((2, 2, *tile_of), F32),
+            pltpu.VMEM((2, LANES), F32),
+            pltpu.VMEM((n_seq, 2, LANES), F32),
+            pltpu.VMEM((1, LANES), F32),
+            pltpu.VMEM((n_feat, 1, LANES), F32),
+            pltpu.SMEM((seq_dev,), jnp.int32),
+            pltpu.SMEM((seq_dev,), jnp.int32),
+            pltpu.SemaphoreType.DMA((20,)),
             pltpu.SemaphoreType.DMA((2, SIDE, 6)),
             pltpu.SemaphoreType.DMA((2, SIDE, 6)),
             pltpu.SemaphoreType.DMA((2, 6)),
             pltpu.SemaphoreType.DMA((2, 6)),
             pltpu.SemaphoreType.DMA((2,)),
             pltpu.SemaphoreType.DMA((2,)),
+            pltpu.SemaphoreType.REGULAR((4,)),
         ],
         compiler_params=pltpu.CompilerParams(collective_id=0, has_side_effects=True, vmem_limit_bytes=60 * 1024 * 1024),
         name="scores",

time: 49.1 us -> 43.4 us (0.88)
  Pallas kernels: 47.7 us -> 42.7 us
  local copies, waits for them, and re-layouts: 1.28 us -> 0.6 us
    pallas_call x1, Pallas kernels: 47.7 us -> 42.7 us  [on_device(): pl.pallas_call(functools.partial(kernel, n_seq), out_shape=pltpu.VMEM((se...]
    unnamed x1, local copies, waits for them, and re-layouts: 1.28 us -> 0.6 us
where the time goes in v2:
time: 43.4 us; the launch traced here: 43.3 us
  Pallas kernels  42.7 us (98%)
  local copies, waits for them, and re-layouts  0.6 us (1%)
    pallas_call x1, Pallas kernels, on_device(): pl.pallas_call(functools.partial(kernel, n_seq), out_shape=pltpu.VMEM((se...  42.7 us

profile of v2, /device:TPU:1, one launch (start us, length us, event | category | flops | bytes accessed | tf_op | source)
XLA Modules:
  0.0 43.3 jit_solution(16876279529143671542)
XLA Ops:
  0.0 42.7 %scores.1 = f32[8,16]{1,0:T(8,128)S(1)} custom-call(s32[8]{0:T(128)} %lengths_hbm.1, s32[8]{0:T(128)} %order_hbm.1, bf16[8,256,512]{2,1,0:T(8,128)(2,1)} %li.1, bf16[8,256,1792]{2,1,0:T(8,128)(2,1)} %og.1, bf16[512,512]{1,0:T(8,128)(2,1)} %qi.1, bf16[1792,512]{1,0:T(8,128)(2,1)} %qo.1), custom_call_target="tpu_custom_call" | custom-call | tf_op jit(solution)/shard_map/scores/pallas_call | solution.py:336
  42.7 0.6 %copy.8 = f32[8,16]{1,0:T(8,128)} copy(f32[8,16]{1,0:T(8,128)S(1)} %scores.1) | data formatting | bytes 1024

commit v3 on v2

--- a/solution.py
+++ b/solution.py
@@ -19,13 +19,14 @@
 
 def kernel(n_seq, lengths_hbm, order_hbm, li, og, qi, qo, out,
            xb, gb, wi, wo, part, rec1, acc1, mid, rec2, acc2, early, tile, gz, mine, gp, lengths, row_order,
-           load_sem, s1_send, s1_recv, s2_send, s2_recv, gz_sem, gp_sem, known):
+           load_sem, sent_sem, s1_recv, s2_recv, gz_sem, gp_sem, known):
     n_feat = SIDE * SIDE
     me_s = lax.axis_index("seq")
     me_f = lax.axis_index("feat")
     y = me_f // SIDE
     x = me_f % SIDE
     rows = xb.shape[2]
+    last = SIDE - 1
     seq_dev = li.shape[0]
 
     def neighbour(axis, step):
@@ -54,23 +55,23 @@
     def tell(r):
         if r < rounds:
             for target in above_below:
-                signal(known.at[r], target)
+                signal(known.at[r % 2], target)
 
     def heard(r):
         if r < rounds:
-            pl.semaphore_wait(known.at[r], 2)
+            pl.semaphore_wait(known.at[r % 2], 2)
 
     def seq_of(h, t):
         return h * SIDE + lax.rem(pos[1 - h] + OFFS[t], SIDE)
 
-    load_lengths = pltpu.make_async_copy(lengths_hbm, lengths, load_sem.at[18])
-    load_order = pltpu.make_async_copy(order_hbm, row_order, load_sem.at[19])
+    load_lengths = pltpu.make_async_copy(lengths_hbm, lengths, load_sem.at[2 + 2 * SIDE])
+    load_order = pltpu.make_async_copy(order_hbm, row_order, load_sem.at[3 + 2 * SIDE])
 
     def load_x(h, t):
-        return pltpu.make_async_copy(li.at[seq_of(h, t)], xb.at[h, t], load_sem.at[2 + h * 8 + t * 2])
+        return pltpu.make_async_copy(li.at[seq_of(h, t)], xb.at[t, h], load_sem.at[2 + t])
 
     def load_g(h, t):
-        return pltpu.make_async_copy(og.at[seq_of(h, t)], gb.at[h, t], load_sem.at[3 + h * 8 + t * 2])
+        return pltpu.make_async_copy(og.at[seq_of(h, t)], gb.at[t, h], load_sem.at[2 + SIDE + t])
 
     load_wi = pltpu.make_async_copy(qi, wi, load_sem.at[0])
     load_wo = pltpu.make_async_copy(qo, wo, load_sem.at[1])
@@ -80,9 +81,6 @@
     load_wo.start()
     load_g(0, 0).start()
     load_g(1, 0).start()
-    for h in range(2):
-        load_x(h, 1).start()
-        load_g(h, 1).start()
 
     def send(src, dst, ssem, rsem, target):
         copy = pltpu.make_async_remote_copy(
@@ -92,13 +90,20 @@
 
     def ring_copy(axis, slot, src, rec, ssem, rsem):
         step = 1 if slot in (0, 2, 5) else SIDE - 1
-        return send(src, rec.at[slot], ssem.at[slot], rsem.at[slot], neighbour(axis, step))
+        return send(src, rec.at[slot], ssem, rsem, neighbour(axis, step))
 
     def tile_in(h, t, step):
         return part.at[h, t, lax.rem(pos[h] + step, SIDE)]
 
     def tile_out(h, t, step):
         return part.at[h, t, SIDE + lax.rem(pos[h] + step, SIDE)]
+
+    def sem1(h, t, slot):
+        kind = (2, 2, 0, 1, 2, 2)[slot] + (1 if t == last and slot >= 4 else 0)
+        return s1_recv.at[h * (3 * SIDE + 1) + 3 * t + kind]
+
+    def sem2(h, slot):
+        return s2_recv.at[h * 3 + (2, 2, 0, 1, 2, 2)[slot]]
 
     def copy1(h, t, slot):
         if slot >= 4:
@@ -107,11 +112,19 @@
             src = tile_in(h, t, 1 if slot == 0 else 2)
         else:
             src = tile_out(h, t, 3 if slot == 1 else 2)
-        return ring_copy(h, slot, src, rec1.at[h, t], s1_send.at[h, t], s1_recv.at[h, t])
+        return ring_copy(h, slot, src, rec1.at[h, t], sent_sem.at[0], sem1(h, t, slot))
 
     def copy2(h, slot):
         src = (mid.at[h, 1, 0], mid.at[h, 2, 1], mid.at[h, 0, 1], mid.at[h, 0, 0], acc2.at[h, 0], acc2.at[h, 1])[slot]
-        return ring_copy(1 - h, slot, src, rec2.at[h], s2_send.at[h], s2_recv.at[h])
+        return ring_copy(1 - h, slot, src, rec2.at[h], sent_sem.at[1], sem2(h, slot))
+
+    def arrived(ref, sem):
+        pltpu.make_async_remote_copy(
+            src_ref=ref, dst_ref=ref, send_sem=sem, recv_sem=sem,
+            device_id={"feat": me_f}, device_id_type=pl.DeviceIdType.MESH).wait_recv()
+
+    def arrived1(h, t):
+        arrived(rec1.at[h, t, pl.ds(0, 4)], sem1(h, t, 0))
 
     def added(*refs):
         total = refs[0][...].astype(F32)
@@ -120,14 +133,16 @@
         return total
 
     def compute_in(h, t):
-        load_x(h, t).wait()
-        value = jnp.dot(xb[h, t], wi[...], preferred_element_type=F32).astype(BF16)
+        if h == 0:
+            pltpu.make_async_copy(xb.at[t], xb.at[t], load_sem.at[2 + t]).wait()
+        value = jnp.dot(xb[t, h], wi[...], preferred_element_type=F32).astype(BF16)
         for c in range(SIDE):
             part[h, t, c] = value[:, c * LANES:(c + 1) * LANES]
 
     def compute_out(h, t):
-        load_g(h, t).wait()
-        value = jnp.dot(gb[h, t], wo[...], preferred_element_type=F32).astype(BF16)
+        if h == 0:
+            pltpu.make_async_copy(gb.at[t], gb.at[t], load_sem.at[2 + SIDE + t]).wait()
+        value = jnp.dot(gb[t, h], wo[...], preferred_element_type=F32).astype(BF16)
         for c in range(SIDE):
             part[h, t, SIDE + c] = value[:, c * LANES:(c + 1) * LANES]
 
@@ -140,22 +155,17 @@
         copy1(h, t, 5).start()
 
     def final1(h, t):
-        copy1(h, t, 0).wait_recv()
-        copy1(h, t, 4).wait_recv()
+        arrived1(h, t)
         mid[h, t, 0] = added(tile_in(h, t, 0), rec1.at[h, t, 0], rec1.at[h, t, 4]).astype(BF16)
-        copy1(h, t, 1).wait_recv()
-        copy1(h, t, 5).wait_recv()
         mid[h, t, 1] = added(tile_out(h, t, 0), rec1.at[h, t, 1], rec1.at[h, t, 5]).astype(BF16)
 
-    def send_in(t):
-        for h in range(2):
-            copy1(h, t, 3).start()
-            copy1(h, t, 0).start()
-
-    def send_out(t):
-        for h in range(2):
-            copy1(h, t, 2).start()
-            copy1(h, t, 1).start()
+    def send_in(h, t):
+        copy1(h, t, 3).start()
+        copy1(h, t, 0).start()
+
+    def send_out(h, t):
+        copy1(h, t, 2).start()
+        copy1(h, t, 1).start()
 
     def load_later(t):
         for h in range(2):
@@ -163,24 +173,26 @@
             load_g(h, t).start()
 
     load_wi.wait()
-    for h in range(2):
-        compute_in(h, 0)
+    compute_in(0, 0)
     pl.semaphore_wait(barrier, len(nearby))
-    send_in(0)
+    send_in(0, 0)
+    compute_in(1, 0)
+    send_in(1, 0)
+    load_later(1)
     tell(0)
     load_wo.wait()
     for h in range(2):
         compute_out(h, 0)
-    send_out(0)
+        send_out(h, 0)
     load_later(2)
     load_lengths.start()
     load_order.start()
     for h in range(2):
         compute_in(h, 1)
-    send_in(1)
+        send_in(h, 1)
     for h in range(2):
         compute_out(h, 1)
-    send_out(1)
+        send_out(h, 1)
     load_later(3)
     heard(0)
     tell(1)
@@ -188,10 +200,10 @@
         accumulate1(h, 0)
     for h in range(2):
         compute_in(h, 2)
-    send_in(2)
+        send_in(h, 2)
     for h in range(2):
         compute_out(h, 2)
-    send_out(2)
+        send_out(h, 2)
     heard(1)
     tell(2)
     for h in range(2):
@@ -207,8 +219,9 @@
         compute_out(h, 3)
     for h in range(2):
         accumulate1(h, 2)
-    send_in(3)
-    send_out(3)
+    for h in range(2):
+        send_in(h, 3)
+        send_out(h, 3)
     for h in range(2):
         final1(h, 1)
         copy2(h, 0).start()
@@ -225,14 +238,10 @@
     for h in range(2):
         accumulate1(h, 3)
     for h in range(2):
-        for side, own in enumerate((tile_in(h, 3, 0), tile_out(h, 3, 0))):
-            copy1(h, 3, side).wait_recv()
-            copy2(h, side).wait_recv()
-            early[h, side] = added(own, rec1.at[h, 3, side], rec2.at[h, side])
-    for h in range(2):
-        for side in range(2):
-            copy2(h, 4 + side).wait_recv()
-            early[h, side] = added(early.at[h, side], rec2.at[h, 4 + side])
+        arrived(rec1.at[h, last, pl.ds(0, 2)], sem1(h, last, 0))
+        arrived(rec2.at[h, pl.ds(0, 4)], sem2(h, 0))
+        for side, own in enumerate((tile_in(h, last, 0), tile_out(h, last, 0))):
+            early[h, side] = added(own, rec1.at[h, last, side], rec2.at[h, side], rec2.at[h, 4 + side])
     heard(3)
     load_lengths.wait()
     load_order.wait()
@@ -242,8 +251,7 @@
     sums = jnp.zeros((SUBLANES, LANES), F32)
     for h in range(2):
         live = row < lengths[seq_of(h, 3)]
-        copy1(h, 3, 4).wait_recv()
-        copy1(h, 3, 5).wait_recv()
+        arrived(rec1.at[h, last, pl.ds(4, 2)], sem1(h, last, 4))
         products = added(early.at[h, 0], rec1.at[h, 3, 4]) * added(early.at[h, 1], rec1.at[h, 3, 5])
         column_sums = jnp.sum(jnp.where(live, products, 0.0), axis=0, keepdims=True)
         sums = jnp.where(slot_row == h, column_sums, sums)
@@ -288,12 +296,10 @@
         if dz or flip:
             if n_seq > 1:
                 spread_z(dz, flip).start()
-    for h in range(2):
-        for t in range(SIDE):
-            for slot in range(6):
-                copy1(h, t, slot).wait_send()
-        for slot in range(6):
-            copy2(h, slot).wait_send()
+    for ref, sem in ((rec1, sent_sem.at[0]), (rec2, sent_sem.at[1])):
+        pltpu.make_async_remote_copy(
+            src_ref=ref, dst_ref=ref, send_sem=sem, recv_sem=sem,
+            device_id={"feat": me_f}, device_id_type=pl.DeviceIdType.MESH).wait_send()
     one_lane = lax.broadcasted_iota(jnp.int32, (1, LANES), 1) // Q
     picks = []
     for i in range(seq_dev):
@@ -339,8 +345,8 @@
         in_specs=[hbm] * 6,
         out_specs=pl.BlockSpec(memory_space=pltpu.VMEM),
         scratch_shapes=[
-            pltpu.VMEM((2, SIDE, rows, width_in), BF16),
-            pltpu.VMEM((2, SIDE, rows, width_out), BF16),
+            pltpu.VMEM((SIDE, 2, rows, width_in), BF16),
+            pltpu.VMEM((SIDE, 2, rows, width_out), BF16),
             pltpu.VMEM((width_in, columns), BF16),
             pltpu.VMEM((width_out, columns), BF16),
             pltpu.VMEM((2, SIDE, 2 * SIDE, *tile_of), BF16),
@@ -356,14 +362,13 @@
             pltpu.VMEM((n_feat, 1, LANES), F32),
             pltpu.SMEM((seq_dev,), jnp.int32),
             pltpu.SMEM((seq_dev,), jnp.int32),
-            pltpu.SemaphoreType.DMA((20,)),
-            pltpu.SemaphoreType.DMA((2, SIDE, 6)),
-            pltpu.SemaphoreType.DMA((2, SIDE, 6)),
-            pltpu.SemaphoreType.DMA((2, 6)),
-            pltpu.SemaphoreType.DMA((2, 6)),
+            pltpu.SemaphoreType.DMA((4 + 2 * SIDE,)),
+            pltpu.SemaphoreType.DMA((2,)),
+            pltpu.SemaphoreType.DMA((2 * (3 * SIDE + 1),)),
+            pltpu.SemaphoreType.DMA((6,)),
             pltpu.SemaphoreType.DMA((2,)),
             pltpu.SemaphoreType.DMA((2,)),
-            pltpu.SemaphoreType.REGULAR((4,)),
+            pltpu.SemaphoreType.REGULAR((2,)),
         ],
         compiler_params=pltpu.CompilerParams(collective_id=0, has_side_effects=True, vmem_limit_bytes=60 * 1024 * 1024),
         name="scores",

time: 43.4 us -> 42.8 us (0.986)
  Pallas kernels: 42.7 us -> 42.1 us
    pallas_call x1, Pallas kernels: 42.7 us -> 42.1 us  [on_device(): pl.pallas_call(functools.partial(kernel, n_seq), out_shape=pltpu.VMEM((se...]
where the time goes in v3:
time: 42.8 us; the launch traced here: 42.7 us
  Pallas kernels  42.1 us (98%)
  local copies, waits for them, and re-layouts  0.6 us (1%)
    pallas_call x1, Pallas kernels, on_device(): pl.pallas_call(functools.partial(kernel, n_seq), out_shape=pltpu.VMEM((se...  42.1 us

profile of v3, /device:TPU:1, one launch (start us, length us, event | category | flops | bytes accessed | tf_op | source)
XLA Modules:
  0.0 42.7 jit_solution(10351145183783864587)
XLA Ops:
  0.0 42.1 %scores.1 = f32[8,16]{1,0:T(8,128)S(1)} custom-call(s32[8]{0:T(128)} %lengths_hbm.1, s32[8]{0:T(128)} %order_hbm.1, bf16[8,256,512]{2,1,0:T(8,128)(2,1)} %li.1, bf16[8,256,1792]{2,1,0:T(8,128)(2,1)} %og.1, bf16[512,512]{1,0:T(8,128)(2,1)} %qi.1, bf16[1792,512]{1,0:T(8,128)(2,1)} %qo.1), custom_call_target="tpu_custom_call" | custom-call | tf_op jit(solution)/shard_map/scores/pallas_call | solution.py:342
  42.1 0.6 %copy.8 = f32[8,16]{1,0:T(8,128)} copy(f32[8,16]{1,0:T(8,128)S(1)} %scores.1) | data formatting | bytes 1024

commit v4 on v3

--- a/solution.py
+++ b/solution.py
@@ -167,6 +167,15 @@
         copy1(h, t, 2).start()
         copy1(h, t, 1).start()
 
+    def far_first(t):
+        for h in range(2):
+            compute_in(h, t)
+            copy1(h, t, 3).start()
+        for h in range(2):
+            compute_out(h, t)
+            for slot in (2, 0, 1):
+                copy1(h, t, slot).start()
+
     def load_later(t):
         for h in range(2):
             load_x(h, t).start()
@@ -187,27 +196,20 @@
     load_later(2)
     load_lengths.start()
     load_order.start()
-    for h in range(2):
-        compute_in(h, 1)
-        send_in(h, 1)
-    for h in range(2):
-        compute_out(h, 1)
-        send_out(h, 1)
+    far_first(1)
     load_later(3)
     heard(0)
     tell(1)
     for h in range(2):
         accumulate1(h, 0)
-    for h in range(2):
-        compute_in(h, 2)
-        send_in(h, 2)
-    for h in range(2):
-        compute_out(h, 2)
-        send_out(h, 2)
+    far_first(2)
     heard(1)
     tell(2)
     for h in range(2):
         accumulate1(h, 1)
+    for h in range(2):
+        compute_in(h, 3)
+        compute_out(h, 3)
     for h in range(2):
         final1(h, 0)
         copy2(h, 3).start()
@@ -215,26 +217,23 @@
     heard(2)
     tell(3)
     for h in range(2):
-        compute_in(h, 3)
-        compute_out(h, 3)
-    for h in range(2):
         accumulate1(h, 2)
     for h in range(2):
-        send_in(h, 3)
-        send_out(h, 3)
+        for slot in (3, 2, 0, 1):
+            copy1(h, 3, slot).start()
     for h in range(2):
         final1(h, 1)
         copy2(h, 0).start()
-    for h in range(2):
-        copy2(h, 2).wait_recv()
-        acc2[h, 1] = added(mid.at[h, 1, 1], rec2.at[h, 2]).astype(BF16)
-        copy2(h, 5).start()
     for h in range(2):
         final1(h, 2)
         copy2(h, 1).start()
         copy2(h, 3).wait_recv()
         acc2[h, 0] = added(mid.at[h, 2, 0], rec2.at[h, 3]).astype(BF16)
         copy2(h, 4).start()
+    for h in range(2):
+        copy2(h, 2).wait_recv()
+        acc2[h, 1] = added(mid.at[h, 1, 1], rec2.at[h, 2]).astype(BF16)
+        copy2(h, 5).start()
     for h in range(2):
         accumulate1(h, 3)
     for h in range(2):
@@ -291,8 +290,8 @@
     def hops(d, size):
         return min(d, size - d)
 
-    far_first = sorted(((hops(dz, n_z), flip, dz) for dz in range(n_z) for flip in range(2)), reverse=True)
-    for _, flip, dz in far_first:
+    order = sorted(((hops(dz, n_z), flip, dz) for dz in range(n_z) for flip in range(2)), reverse=True)
+    for _, flip, dz in order:
         if dz or flip:
             if n_seq > 1:
                 spread_z(dz, flip).start()
@@ -315,8 +314,8 @@
         packed = jnp.where(one_lane == place, gz[who, pl.ds(half, 1), :], packed)
     mine[...] = packed
     gp[me_f] = packed
-    far_first = sorted(((hops(dy, SIDE) + hops(dx, SIDE), dy, dx) for dy in range(SIDE) for dx in range(SIDE)), reverse=True)
-    for _, dy, dx in far_first[:-1]:
+    order = sorted(((hops(dy, SIDE) + hops(dx, SIDE), dy, dx) for dy in range(SIDE) for dx in range(SIDE)), reverse=True)
+    for _, dy, dx in order[:-1]:
         spread_plane(dy, dx).start()
     if n_seq > 1:
         all_of(gz, gz_sem, n_seq - 1, "seq").wait_send()

time: 42.8 us -> 42.6 us (level)
  no operation moved by 1% of the time
where the time goes in v4:
time: 42.6 us; the launch traced here: 42.5 us
  Pallas kernels  41.9 us (98%)
  local copies, waits for them, and re-layouts  0.6 us (1%)
    pallas_call x1, Pallas kernels, on_device(): pl.pallas_call(functools.partial(kernel, n_seq), out_shape=pltpu.VMEM((se...  41.9 us

profile of v4, /device:TPU:1, one launch (start us, length us, event | category | flops | bytes accessed | tf_op | source)
XLA Modules:
  0.0 42.5 jit_solution(10190343375543422940)
XLA Ops:
  0.0 41.9 %scores.1 = f32[8,16]{1,0:T(8,128)S(1)} custom-call(s32[8]{0:T(128)} %lengths_hbm.1, s32[8]{0:T(128)} %order_hbm.1, bf16[8,256,512]{2,1,0:T(8,128)(2,1)} %li.1, bf16[8,256,1792]{2,1,0:T(8,128)(2,1)} %og.1, bf16[512,512]{1,0:T(8,128)(2,1)} %qi.1, bf16[1792,512]{1,0:T(8,128)(2,1)} %qo.1), custom_call_target="tpu_custom_call" | custom-call | tf_op jit(solution)/shard_map/scores/pallas_call | solution.py:341
  41.9 0.6 %copy.8 = f32[8,16]{1,0:T(8,128)} copy(f32[8,16]{1,0:T(8,128)S(1)} %scores.1) | data formatting | bytes 1024
